TPU v7x, 512 devices: a whole 4x4x16 slice. The times are simulated.
512 devices in a mesh: tm: 16 (over z_lo, x), chan: 32 (over z_hi, y, core).
Axes of the slice: x: 4, y: 4, z: 16 (z_hi: 4, z_lo: 4; z = z_hi * 4 + z_lo), core: 2. Of those that a mesh axis runs over, the one named last changes fastest.
Arguments:
- voltages: bfloat16 [2, 128, 2048, 1024], P(None, 'tm', 'chan'), may hold values from -6 to 6
- subspace: float32 [32, 64, 32, 1024], P('chan', 'tm'), may hold values from -0.1875 to 0.1875
- order: int32 [64], replicated, may hold values from 0 to 63, each once
- beam_seeds: int32 [256], replicated, may hold values from 1 to 65520
- flagged: int32 [16], replicated, may hold values from 0 to 511
Outputs:
- beams: bfloat16 [2, 32, 64, 512, 128], P(None, None, 'tm', 'chan')
- tracked: float32 [32, 64, 32, 1024], P('chan', 'tm')
Inputs may be any that keep to these rules, and one draw needn't show every extreme that they name: `order`: each of 0 to 63 once. `flagged`: station numbers; a station may occur more than once.
All inputs are finite; a program needn't handle non-finite values.
Results may differ from a plain program's by a relative error of at most 0.0084.
Values may be sent and summed in bfloat16 or wider, within the bound.
No kernel may reach another device: no remote copies, remote signals or barrier semaphores. Data moves between devices by JAX's collectives and lax.ppermute only.
A program may use at most 64 MiB of HBM per device.

v0:
```python
import math

import jax
import jax.numpy as jnp
from jax import lax
from jax.sharding import PartitionSpec as P

CH = 2048
SUB = 2


TWO_PI = 2.0 * math.pi


def beam_weights(beam_seeds, channels, stations, total_channels):
    station_no = jnp.arange(stations, dtype=jnp.int32) + 1
    delays = (station_no[:, None] * beam_seeds[None, :] % 65521).astype(jnp.float32) / 65521.0
    frequency = 1.0 + channels.astype(jnp.float32) / total_channels
    angles = delays[None, :, :] * (TWO_PI * frequency)[:, None, None]
    factor = 1.0 / math.sqrt(stations)
    cosine = jnp.cos(angles) * factor
    sine_part = jnp.sin(angles) * factor
    upper = jnp.concatenate([cosine, sine_part], axis=2)
    under = jnp.concatenate([-sine_part, cosine], axis=2)
    return jnp.concatenate([upper, under], axis=1).astype(jnp.bfloat16)


def power_step(voltage_input, tracked, steering_weight):
    sample_count = voltage_input.shape[0]
    coarse_channel = tracked.astype(jnp.bfloat16)
    projected_input = jnp.einsum(
        "xbj,bqj->bxq", voltage_input, coarse_channel, preferred_element_type=jnp.float32
    ).astype(jnp.bfloat16)
    beam_image = (
        jnp.einsum(
            "nwg,wny->ngy", projected_input, voltage_input, preferred_element_type=jnp.float32
        )
        + sample_count * tracked
    )
    gram = jnp.einsum("crs,cks->crk", beam_image, beam_image, precision=lax.Precision.HIGHEST)
    lower = jnp.linalg.cholesky(gram)
    tracked = jax.scipy.linalg.solve_triangular(lower, beam_image, lower=True)
    subspace_vectors = tracked.astype(jnp.bfloat16)
    lengthwise_axis = jnp.einsum(
        "xbj,bqj->bxq", voltage_input, subspace_vectors, preferred_element_type=jnp.float32
    ).astype(jnp.bfloat16)
    mixing = jnp.einsum(
        "crs,csb->crb", subspace_vectors, steering_weight, preferred_element_type=jnp.float32
    ).astype(jnp.bfloat16)
    direct_output = jnp.einsum(
        "edi,diy->dye", voltage_input, steering_weight, preferred_element_type=jnp.float32
    )
    beams = direct_output - jnp.einsum(
        "ctr,crb->cbt", lengthwise_axis, mixing, preferred_element_type=jnp.float32
    )
    return (tracked, beams.astype(jnp.bfloat16))


def per_device(voltages, subspace, order, beam_seeds, flagged):
    signals = voltages.shape[-1]
    stations = signals // 2
    slots = subspace.shape[1]
    per_group = order.shape[0]
    marks = jnp.any(flagged[:, None] == jnp.arange(stations, dtype=jnp.int32)[None, :], axis=0)
    keep = jnp.where(marks, 0.0, 1.0).astype(jnp.bfloat16)
    keep = jnp.concatenate([keep, keep])
    ordered = jnp.take(voltages, order, axis=2) * keep
    group = lax.axis_index("chan")
    first_slot = lax.axis_index("tm") * slots
    chosen = lax.dynamic_slice_in_dim(order, first_slot, slots)
    channels = group * per_group + chosen
    steering_weight = beam_weights(beam_seeds, channels, stations, CH)
    state = subspace[0]
    results = []
    for part in range(SUB):
        turned = lax.all_to_all(ordered[part], "tm", split_axis=1, concat_axis=0, tiled=True)
        state, formed = power_step(turned, state, steering_weight)
        results.append(
            lax.all_to_all(formed[None], "chan", split_axis=2, concat_axis=0, tiled=True)
        )
    output = jnp.stack(results)
    return (output, state[None])


def solution(mesh):
    return jax.shard_map(
        per_device,
        mesh=mesh,
        in_specs=(P(None, "tm", "chan", None), P("chan", "tm", None, None), P(), P(), P()),
        out_specs=(P(None, None, "tm", "chan", None), P("chan", "tm", None, None)),
        check_vma=False,
    )
```

profile of v0, /device:TPU:18, one launch (start us, length us, event | category | flops | bytes accessed | tf_op | source)
XLA Modules:
  0.0 211.9 jit_solution(4434291030982119377)
XLA Ops:
  0.6 0.0 copy-start
  0.6 0.8 compare_select_fusion
  1.5 0.7 compare_and_fusion
  2.1 0.7 fusion.50
  2.9 0.0 copy-done
  2.9 7.9 %gather_fusion = bf16[64,2,8,1024]{3,0,2,1:T(8,128)(2,1)} fusion(bf16[2,8,64,1024]{3,2,1,0:T(8,128)(2,1)S(1)} %copy-done, s32[1024]{0:T(1024)S(1)} %pad_clamp_fusion), kind=kCustom, calls=%fused_computation | custom fusion | bytes 4194560 | tf_op jit(solution)/shard_map/jit(_take)/gather | solution.py:67
  10.8 1.8 multiply_bitcast_fusion
  12.7 1.1 slice_bitcast_fusion.1
  13.8 1.5 copy.37
  15.4 8.9 %all-to-all-start = ((bf16[8,64,1024]{2,0,1:T(8,128)(2,1)}), bf16[8,64,1024]{2,0,1:T(8,128)(2,1)S(1)}, u32[]{:S(2)}, u32[]{:S(2)}) async-start(bf16[8,64,1024]{2,0,1:T(8,128)(2,1)} %copy.37), calls=%async_computation | async-start | bytes 2097152 | tf_op jit(solution)/shard_map/all_to_all | solution.py:76
  24.3 0.0 copy-start.12
  24.3 0.0 copy-start.11
  24.3 2.8 %copy.44 = bf16[8,64,1024]{2,0,1:T(8,128)(2,1)} copy(bf16[8,64,1024]{2,1,0:T(8,128)(2,1)} %get-tuple-element.5) | data formatting | bytes 2097152 | tf_op jit(solution)/shard_map/squeeze | solution.py:76
  27.1 20.1 %all-to-all-done = bf16[8,64,1024]{2,0,1:T(8,128)(2,1)S(1)} async-done(((bf16[8,64,1024]{2,0,1:T(8,128)(2,1)}), bf16[8,64,1024]{2,0,1:T(8,128)(2,1)S(1)}, u32[]{:S(2)}, u32[]{:S(2)}) %all-to-all-start) | async-done | bytes 1048608 | tf_op jit(solution)/shard_map/all_to_all | solution.py:76
  47.2 1.0 copy-done.1
  48.2 8.0 %all-to-all-start.2 = ((bf16[8,64,1024]{2,0,1:T(8,128)(2,1)}), bf16[8,64,1024]{2,0,1:T(8,128)(2,1)S(1)}, u32[]{:S(2)}, u32[]{:S(2)}) async-start(bf16[8,64,1024]{2,0,1:T(8,128)(2,1)} %copy.44), calls=%async_computation.2 | async-start | bytes 2097152 | tf_op jit(solution)/shard_map/all_to_all | solution.py:76
  56.1 0.0 copy-done.12
  56.1 0.1 add_multiply_fusion
  56.2 0.0 copy-done.11
  56.3 0.4 fusion.33
  56.6 9.1 %fusion.4 = (bf16[4,512,256]{1,2,0:T(8,128)(2,1)}, bf16[4,512,256]{1,2,0:T(8,128)(2,1)}, bf16[4,512,256]{1,2,0:T(8,128)(2,1)}) fusion(f32[4]{0:T(128)S(1)} %add_multiply_fusion, f32[512,256]{0,1:T(8,128)S(1)} %fusion.33), kind=kLoop, calls=%fused_computation.8 | loop fusion | flops 3670016 | bytes 3670032 | tf_op jit(solution)/shard_map/convert.5
  65.8 3.3 %convolution_add_fusion.1 = f32[4,32,1024]{2,1,0:T(8,128)} fusion(bf16[8,16,4,1024]{3,0,2,1:T(8,128)(2,1)} %bitcast.82, f32[1,4,32,1024]{3,2,1,0:T(8,128)} %param.9), kind=kOutput, calls=%fused_computation.18 | convolution fusion | flops 67518464 | bytes 2097152 | tf_op jit(solution)/shard_map/nwg,wny->ngy/dot_general | solution.py:35
  69.0 1.8 fusion.56
  70.9 0.1 copy.39
  71.0 11.7 %custom-call.8 = f32[4,32,32]{2,1,0:T(8,128)S(1)} custom-call(f32[4,32,32]{2,1,0:T(8,128)S(1)} %fusion.49), custom_call_target="Cholesky" | custom-call | tf_op jit(solution)/shard_map/jit(cholesky)/cholesky | solution.py:41
  82.7 0.1 compare_reduce_fusion.1
  82.9 0.1 select_bitcast_fusion.1
  83.0 9.8 %custom-call.9 = f32[4,1,32,32]{2,3,1,0:T(8,128)S(1)} custom-call(f32[4,1,32,32]{3,2,1,0:T(8,128)S(1)} %select_bitcast_fusion.1), custom_call_target="InvertDiagBlocksLowerTriangular" | custom-call | tf_op jit(solution)/shard_map/jit(_solve_triangular)/vmap()/triangular_solve | solution.py:42
  92.8 1.7 fusion.47
  94.5 0.0 copy-start.3
  94.5 0.8 copy-done.3
  95.3 3.7 %convolution_convert_fusion.1 = bf16[4,32,512]{2,1,0:T(8,128)(2,1)S(1)} fusion(f32[4,32,1024]{2,1,0:T(8,128)S(1)} %fusion.47, bf16[4,512,256]{1,2,0:T(8,128)(2,1)} %get-tuple-element.8, bf16[4,512,256]{1,2,0:T(8,128)(2,1)} %get-tuple-element.7, bf16[4,512,256]{1,2,0:T(8,128)(2,1)} %get-tuple-element.6), kind=kOutput, calls=%fused_computation.20 | convolution fusion | flops 151191552 | bytes 3801088 | tf_op jit(solution)/shard_map/crs,csb->crb/dot_general | solution.py:47
  99.0 0.0 copy-done.2
  99.0 0.0 copy-done.5
  99.0 0.0 copy-done.7
  99.0 0.0 copy-done.9
  99.0 2.2 %fusion.20 = f32[4,512,128]{2,1,0:T(8,128)} fusion(bf16[8,16,4,1024]{3,0,2,1:T(8,128)(2,1)S(1)} %bitcast.84, bf16[4,512,256]{1,2,0:T(8,128)(2,1)S(1)} %copy-done.9, bf16[4,512,256]{1,2,0:T(8,128)(2,1)S(1)} %copy-done.7, bf16[4,512,256]{1,2,0:T(8,128)(2,1)S(1)} %copy-done.5), kind=kOutput, calls=%fused_computation.34 | convolution fusion | flops 553648128 | bytes 5242880 | tf_op jit(solution)/shard_map/edi,diy->dye/dot_general | solution.py:50
  101.3 3.2 %fusion.9 = bf16[1,4,512,128]{3,2,1,0:T(8,128)(2,1)} fusion(f32[4,512,128]{2,1,0:T(8,128)} %fusion.20, bf16[4,32,512]{2,1,0:T(8,128)(2,1)S(1)} %convolution_convert_fusion.1, bf16[8,16,4,1024]{3,0,2,1:T(8,128)(2,1)} %bitcast.83, f32[4,32,1024]{2,1,0:T(8,128)} %copy-done.3), kind=kOutput, calls=%fused_computation.16 | convolution fusion | flops 51003392 | bytes 3276800 | tf_op jit(solution)/shard_map/ctr,crb->cbt/dot_general | solution.py:53
  104.5 2.2 %copy.42 = bf16[1,4,512,128]{3,1,0,2:T(4,128)(2,1)} copy(bf16[1,4,512,128]{3,2,1,0:T(8,128)(2,1)} %fusion.9) | data formatting | bytes 1048576 | tf_op jit(solution)/shard_map/broadcast_in_dim | solution.py:79
  106.8 0.0 all-to-all-done.2
  106.8 15.6 %all-to-all-start.1 = ((bf16[1,4,512,128]{3,1,0,2:T(4,128)(2,1)}), bf16[1,4,512,128]{3,1,0,2:T(4,128)(2,1)}, u32[]{:S(2)}, u32[]{:S(2)}) async-start(bf16[1,4,512,128]{3,1,0,2:T(4,128)(2,1)} %copy.42), calls=%async_computation.1 | async-start | bytes 1048576 | tf_op jit(solution)/shard_map/all_to_all | solution.py:79
  122.3 2.7 %convolution_add_fusion = f32[4,32,1024]{2,1,0:T(8,128)} fusion(bf16[8,16,4,1024]{3,0,2,1:T(8,128)(2,1)S(1)} %bitcast.79, f32[4,32,1024]{2,1,0:T(8,128)} %copy-done.3), kind=kOutput, calls=%fused_computation.17 | convolution fusion | flops 67518464 | bytes 2097152 | tf_op jit(solution)/shard_map/nwg,wny->ngy/dot_general | solution.py:35
  125.0 1.8 fusion.57
  126.9 0.1 copy.46
  127.0 11.7 %custom-call.10 = f32[4,32,32]{2,1,0:T(8,128)S(1)} custom-call(f32[4,32,32]{2,1,0:T(8,128)S(1)} %fusion.46), custom_call_target="Cholesky" | custom-call | tf_op jit(solution)/shard_map/jit(cholesky)/cholesky | solution.py:41
  138.8 0.1 compare_reduce_fusion
  138.9 0.1 select_bitcast_fusion
  139.0 9.8 %custom-call.11 = f32[4,1,32,32]{2,3,1,0:T(8,128)S(1)} custom-call(f32[4,1,32,32]{3,2,1,0:T(8,128)S(1)} %select_bitcast_fusion), custom_call_target="InvertDiagBlocksLowerTriangular" | custom-call | tf_op jit(solution)/shard_map/jit(_solve_triangular)/vmap()/triangular_solve | solution.py:42
  148.8 1.7 fusion.44
  150.5 0.0 copy-start.4
  150.5 0.8 copy-done.4
  151.3 3.7 %convolution_convert_fusion = bf16[4,32,512]{2,1,0:T(8,128)(2,1)S(1)} fusion(f32[4,32,1024]{2,1,0:T(8,128)S(1)} %fusion.44, bf16[4,512,256]{1,2,0:T(8,128)(2,1)} %get-tuple-element.8, bf16[4,512,256]{1,2,0:T(8,128)(2,1)} %get-tuple-element.7, bf16[4,512,256]{1,2,0:T(8,128)(2,1)} %get-tuple-element.6), kind=kOutput, calls=%fused_computation.19 | convolution fusion | flops 151191552 | bytes 3801088 | tf_op jit(solution)/shard_map/crs,csb->crb/dot_general | solution.py:47
  155.0 0.0 copy-done.6
  155.0 0.0 copy-done.8
  155.0 0.0 copy-done.10
  155.0 2.3 %fusion.14 = f32[4,512,128]{2,1,0:T(8,128)} fusion(bf16[8,16,4,1024]{3,0,2,1:T(8,128)(2,1)S(1)} %bitcast.80, bf16[4,512,256]{1,2,0:T(8,128)(2,1)S(1)} %copy-done.10, bf16[4,512,256]{1,2,0:T(8,128)(2,1)S(1)} %copy-done.8, bf16[4,512,256]{1,2,0:T(8,128)(2,1)S(1)} %copy-done.6), kind=kOutput, calls=%fused_computation.30 | convolution fusion | flops 553648128 | bytes 5242880 | tf_op jit(solution)/shard_map/edi,diy->dye/dot_general | solution.py:50
  157.3 2.9 %fusion.8 = bf16[1,4,512,128]{3,2,1,0:T(8,128)(2,1)} fusion(f32[4,512,128]{2,1,0:T(8,128)} %fusion.14, bf16[4,32,512]{2,1,0:T(8,128)(2,1)S(1)} %convolution_convert_fusion, bf16[8,16,4,1024]{3,0,2,1:T(8,128)(2,1)S(1)} %bitcast.81, f32[4,32,1024]{2,1,0:T(8,128)} %copy-done.4), kind=kOutput, calls=%fused_computation.15 | convolution fusion | flops 51003392 | bytes 3276800 | tf_op jit(solution)/shard_map/ctr,crb->cbt/dot_general | solution.py:53
  160.2 2.2 %copy.49 = bf16[1,4,512,128]{3,1,0,2:T(4,128)(2,1)} copy(bf16[1,4,512,128]{3,2,1,0:T(8,128)(2,1)} %fusion.8) | data formatting | bytes 1048576 | tf_op jit(solution)/shard_map/broadcast_in_dim | solution.py:79
  162.4 0.0 all-to-all-done.1
  162.4 14.6 %all-to-all-start.3 = ((bf16[1,4,512,128]{3,1,0,2:T(4,128)(2,1)}), bf16[1,4,512,128]{3,1,0,2:T(4,128)(2,1)S(1)}, u32[]{:S(2)}, u32[]{:S(2)}) async-start(bf16[1,4,512,128]{3,1,0,2:T(4,128)(2,1)} %copy.49), calls=%async_computation.3 | async-start | bytes 1048576 | tf_op jit(solution)/shard_map/all_to_all | solution.py:79
  177.0 1.1 copy.90
  178.2 32.6 %all-to-all-done.3 = bf16[1,4,512,128]{3,1,0,2:T(4,128)(2,1)S(1)} async-done(((bf16[1,4,512,128]{3,1,0,2:T(4,128)(2,1)}), bf16[1,4,512,128]{3,1,0,2:T(4,128)(2,1)S(1)}, u32[]{:S(2)}, u32[]{:S(2)}) %all-to-all-start.3) | async-done | bytes 524320 | tf_op jit(solution)/shard_map/all_to_all | solution.py:79
  210.8 0.1 copy.89
  210.8 1.1 pad_maximum_fusion
  (18 shorter events, 0.1 us)
Async XLA Ops:
  0.6 2.3 %copy-start = (bf16[2,8,64,1024]{3,2,1,0:T(8,128)(2,1)S(1)}, bf16[2,8,64,1024]{3,2,1,0:T(8,128)(2,1)}, u32[]{:S(2)}) copy-start(bf16[2,8,64,1024]{3,2,1,0:T(8,128)(2,1)} %param.8) | copy-start | bytes 6291460
  15.4 31.8 %all-to-all-start = ((bf16[8,64,1024]{2,0,1:T(8,128)(2,1)}), bf16[8,64,1024]{2,0,1:T(8,128)(2,1)S(1)}, u32[]{:S(2)}, u32[]{:S(2)}) async-start(bf16[8,64,1024]{2,0,1:T(8,128)(2,1)} %copy.37), calls=%async_computation | async-start | bytes 2097152 | tf_op jit(solution)/shard_map/all_to_all | solution.py:76
  24.3 31.9 %copy-start.12 = (s32[64]{0:T(128)S(1)}, s32[64]{0:T(128)}, u32[]{:S(2)}) copy-start(s32[64]{0:T(128)} %param.10) | copy-start | bytes 772
  24.3 32.0 %copy-start.11 = (s32[256]{0:T(256)S(1)}, s32[256]{0:T(256)}, u32[]{:S(2)}) copy-start(s32[256]{0:T(256)} %param.11) | copy-start | bytes 3076
  47.2 1.0 copy-start.1
  48.2 58.6 %all-to-all-start.2 = ((bf16[8,64,1024]{2,0,1:T(8,128)(2,1)}), bf16[8,64,1024]{2,0,1:T(8,128)(2,1)S(1)}, u32[]{:S(2)}, u32[]{:S(2)}) async-start(bf16[8,64,1024]{2,0,1:T(8,128)(2,1)} %copy.44), calls=%async_computation.2 | async-start | bytes 2097152 | tf_op jit(solution)/shard_map/all_to_all | solution.py:76
  94.5 0.8 copy-start.3
  95.3 3.7 %copy-start.2 = (bf16[8,64,1024]{2,0,1:T(8,128)(2,1)S(1)}, bf16[8,64,1024]{2,0,1:T(8,128)(2,1)}, u32[]{:S(2)}) copy-start(bf16[8,64,1024]{2,0,1:T(8,128)(2,1)} %copy-done.1) | copy-start | bytes 3145732
  95.3 3.7 %copy-start.5 = (bf16[4,512,256]{1,2,0:T(8,128)(2,1)S(1)}, bf16[4,512,256]{1,2,0:T(8,128)(2,1)}, u32[]{:S(2)}) copy-start(bf16[4,512,256]{1,2,0:T(8,128)(2,1)} %get-tuple-element.6) | copy-start | bytes 3145732
  95.3 3.7 %copy-start.7 = (bf16[4,512,256]{1,2,0:T(8,128)(2,1)S(1)}, bf16[4,512,256]{1,2,0:T(8,128)(2,1)}, u32[]{:S(2)}) copy-start(bf16[4,512,256]{1,2,0:T(8,128)(2,1)} %get-tuple-element.7) | copy-start | bytes 3145732
  95.3 3.7 %copy-start.9 = (bf16[4,512,256]{1,2,0:T(8,128)(2,1)S(1)}, bf16[4,512,256]{1,2,0:T(8,128)(2,1)}, u32[]{:S(2)}) copy-start(bf16[4,512,256]{1,2,0:T(8,128)(2,1)} %get-tuple-element.8) | copy-start | bytes 3145732
  106.8 55.7 %all-to-all-start.1 = ((bf16[1,4,512,128]{3,1,0,2:T(4,128)(2,1)}), bf16[1,4,512,128]{3,1,0,2:T(4,128)(2,1)}, u32[]{:S(2)}, u32[]{:S(2)}) async-start(bf16[1,4,512,128]{3,1,0,2:T(4,128)(2,1)} %copy.42), calls=%async_computation.1 | async-start | bytes 1048576 | tf_op jit(solution)/shard_map/all_to_all | solution.py:79
  150.5 0.8 copy-start.4
  151.3 3.7 %copy-start.6 = (bf16[4,512,256]{1,2,0:T(8,128)(2,1)S(1)}, bf16[4,512,256]{1,2,0:T(8,128)(2,1)}, u32[]{:S(2)}) copy-start(bf16[4,512,256]{1,2,0:T(8,128)(2,1)} %get-tuple-element.6) | copy-start | bytes 3145732
  151.3 3.7 %copy-start.8 = (bf16[4,512,256]{1,2,0:T(8,128)(2,1)S(1)}, bf16[4,512,256]{1,2,0:T(8,128)(2,1)}, u32[]{:S(2)}) copy-start(bf16[4,512,256]{1,2,0:T(8,128)(2,1)} %get-tuple-element.7) | copy-start | bytes 3145732
  151.3 3.7 %copy-start.10 = (bf16[4,512,256]{1,2,0:T(8,128)(2,1)S(1)}, bf16[4,512,256]{1,2,0:T(8,128)(2,1)}, u32[]{:S(2)}) copy-start(bf16[4,512,256]{1,2,0:T(8,128)(2,1)} %get-tuple-element.8) | copy-start | bytes 3145732
  162.4 48.3 %all-to-all-start.3 = ((bf16[1,4,512,128]{3,1,0,2:T(4,128)(2,1)}), bf16[1,4,512,128]{3,1,0,2:T(4,128)(2,1)S(1)}, u32[]{:S(2)}, u32[]{:S(2)}) async-start(bf16[1,4,512,128]{3,1,0,2:T(4,128)(2,1)} %copy.49), calls=%async_computation.3 | async-start | bytes 1048576 | tf_op jit(solution)/shard_map/all_to_all | solution.py:79
where the time goes:
time: 213 us; the launch traced here: 212 us
  other arithmetic  58.4 us (27%)
  waiting for transfers between devices  52.7 us (25%)
  starting transfers between devices  47 us (22%)
  matrix products  31 us (15%)
  local copies, waits for them, and re-layouts  21.9 us (10%)
    all_to_all x2, waiting for transfers between devices, per_device(): lax.all_to_all(formed[None], 'chan', split_axis=2, concat_axis=0, tiled=T...  32.6 us
    all_to_all x2, starting transfers between devices, per_device(): lax.all_to_all(formed[None], 'chan', split_axis=2, concat_axis=0, tiled=T...  30.2 us
    another operation x7, other arithmetic, power_step(): lower = jnp.linalg.cholesky(gram)  23.8 us
    all_to_all x2, waiting for transfers between devices, per_device(): lax.all_to_all(ordered[part], 'tm', split_axis=1, concat_axis=0, tiled=True)  20.1 us
    another operation x5, other arithmetic, power_step(): tracked = jax.scipy.linalg.solve_triangular(lower, beam_image, lower=True)  19.9 us
    all_to_all x2, starting transfers between devices, per_device(): lax.all_to_all(ordered[part], 'tm', split_axis=1, concat_axis=0, tiled=True)  16.9 us
    another operation x1, other arithmetic  9.12 us
    gather x1, local copies, waits for them, and re-layouts, per_device(): ordered = jnp.take(voltages, order, axis=2) * keep  7.92 us
  transfers between devices with their start and end apart: 4, of which 2 were waited for; matrix products, arithmetic and copies ran while one was open for 44% of the time, Pallas kernels for 0%

commit v1 on v0

v1 whole, which is shorter than its diff:
```python
import functools
import math

import jax
import jax.numpy as jnp
import numpy as np
from jax import lax
from jax.experimental import pallas as pl
from jax.experimental.pallas import tpu as pltpu
from jax.sharding import PartitionSpec as P

CH = 2048
SUB = 2
MIB = 1024 * 1024
TRACK_LIMIT = 48 * MIB
NT = (((1,), (1,)), ((), ()))


def half_turn_fits():
    f = 0.5 * np.cos(np.pi * (np.arange(400) + 0.5) / 400)
    square = f * f
    powers = np.stack([square**n for n in range(6)], axis=1)
    sine = np.linalg.lstsq(powers * f[:, None], np.sin(np.pi * f), rcond=None)[0]
    cosine = np.linalg.lstsq(powers, np.cos(np.pi * f), rcond=None)[0]
    return [float(v) for v in sine], [float(v) for v in cosine]


def horner(coefficients, x):
    total = jnp.full_like(x, coefficients[-1])
    for c in reversed(coefficients[:-1]):
        total = total * x + c
    return total


def select_kernel(order_any, flagged_any, x_any, out_any, *scratch):
    order_ref, flagged_ref, x_ref, pick_ref, out_ref, small_sems, in_sems, out_sems = scratch
    parts, times, per_group, signals = x_ref.shape
    owners, _, each, _ = out_any.shape
    rows = times * per_group
    stations = signals // 2
    wide = signals // in_sems.shape[1]
    cuts = [(p, c) for p in range(parts) for c in range(in_sems.shape[1])]
    small = [
        pltpu.make_async_copy(order_any, order_ref, small_sems.at[0]),
        pltpu.make_async_copy(flagged_any, flagged_ref, small_sems.at[1]),
    ]
    for copy in small:
        copy.start()
    loads = []
    for p, c in cuts:
        cut = pl.ds(c * wide, wide)
        loads.append(
            pltpu.make_async_copy(
                x_any.at[p, :, :, cut], x_ref.at[p, :, :, cut], in_sems.at[p, c]
            )
        )
        loads[-1].start()
    for copy in small:
        copy.wait()
    row = lax.broadcasted_iota(jnp.int32, (2 * times, rows), 0)
    column = lax.broadcasted_iota(jnp.int32, (2 * times, rows), 1)
    first = row < times
    base = jnp.where(first, row, row - times) * per_group
    for pair in range(per_group // 2):
        channel = jnp.where(first, order_ref[2 * pair], order_ref[2 * pair + 1])
        hit = jnp.where(column == base + channel, 1.0, 0.0)
        pick_ref[2 * times * pair : 2 * times * (pair + 1), :] = hit.astype(jnp.bfloat16)
    signal = lax.broadcasted_iota(jnp.int32, (8, signals), 1)
    station = jnp.where(signal >= stations, signal - stations, signal)
    dropped = station == flagged_ref[0]
    for entry in range(1, flagged_ref.shape[0]):
        dropped = jnp.logical_or(dropped, station == flagged_ref[entry])
    keep = jnp.where(dropped, 0.0, 1.0)
    stores = []
    for (p, c), load in zip(cuts, loads, strict=True):
        load.wait()
        cut = slice(c * wide, (c + 1) * wide)
        block = x_ref[p, :, :, cut].reshape(rows, wide)
        moved = jnp.dot(pick_ref[...], block, preferred_element_type=jnp.float32)
        moved = (moved * keep[0:1, cut]).astype(jnp.bfloat16)
        out_ref[:, p, :, cut] = moved.reshape(owners, each, wide)
        span = pl.ds(c * wide, wide)
        stores.append(
            pltpu.make_async_copy(
                out_ref.at[:, p, :, span], out_any.at[:, p, :, span], out_sems.at[p, c]
            )
        )
        stores[-1].start()
    for store in stores:
        store.wait()


def select(voltages, order, flagged, owners):
    parts, times, per_group, signals = voltages.shape
    rows = times * per_group
    cuts = 4
    hbm = pl.BlockSpec(memory_space=pltpu.HBM)
    shape = (owners, parts, rows // owners, signals)
    return pl.pallas_call(
        select_kernel,
        in_specs=[hbm] * 3,
        out_specs=hbm,
        out_shape=jax.ShapeDtypeStruct(shape, jnp.bfloat16),
        scratch_shapes=[
            pltpu.SMEM(order.shape, jnp.int32),
            pltpu.SMEM(flagged.shape, jnp.int32),
            pltpu.VMEM(voltages.shape, jnp.bfloat16),
            pltpu.VMEM((rows, rows), jnp.bfloat16),
            pltpu.VMEM(shape, jnp.bfloat16),
            pltpu.SemaphoreType.DMA((2,)),
            pltpu.SemaphoreType.DMA((parts, cuts)),
            pltpu.SemaphoreType.DMA((parts, cuts)),
        ],
        compiler_params=pltpu.CompilerParams(vmem_limit_bytes=67043328),
        cost_estimate=pl.CostEstimate(
            flops=2 * parts * rows * rows * signals,
            bytes_accessed=4 * parts * rows * signals,
            transcendentals=0,
        ),
        name="select_slots",
    )(order, flagged, voltages)


def weights_kernel(fits, channel_ref, seeds_ref, out_ref, delay_ref):
    stations, beams = delay_ref.shape
    factor = 1.0 / math.sqrt(stations)
    sine_fit, cosine_fit = fits

    @pl.when(pl.program_id(0) == 0)
    def _():
        step = 64

        def fill(block, _):
            start = pl.multiple_of(block * step, step)
            number = lax.broadcasted_iota(jnp.int32, (step, beams), 0) + (start + 1)
            product = number * seeds_ref[...]
            whole = jnp.floor(product.astype(jnp.float32) * (1.0 / 65521.0)).astype(jnp.int32)
            rest = product - whole * 65521
            rest = jnp.where(rest < 0, rest + 65521, rest)
            rest = jnp.where(rest >= 65521, rest - 65521, rest)
            delay_ref[pl.ds(start, step), :] = rest.astype(jnp.float32) / 65521.0
            return 0

        lax.fori_loop(0, stations // step, fill, 0)

    frequency = 1.0 + channel_ref[pl.program_id(0)].astype(jnp.float32) * (1.0 / CH)
    double = 2.0 * frequency
    step = 32

    def fill(block, _):
        start = pl.multiple_of(block * step, step)
        turns = delay_ref[pl.ds(start, step), :] * double
        near = jnp.floor(turns + 0.5)
        f = turns - near
        half = near * 0.5
        odd = half - jnp.floor(half)
        amplitude = factor - (4.0 * factor) * odd
        square = f * f
        real = (horner(cosine_fit, square) * amplitude).astype(jnp.bfloat16)
        imaginary = horner(sine_fit, square) * (f * amplitude)
        plus = imaginary.astype(jnp.bfloat16)
        minus = (-imaginary).astype(jnp.bfloat16)
        out_ref[pl.ds(start, step), :beams] = real
        out_ref[pl.ds(start, step), beams:] = plus
        under = pl.multiple_of(stations + start, step)
        out_ref[pl.ds(under, step), :beams] = minus
        out_ref[pl.ds(under, step), beams:] = real
        return 0

    lax.fori_loop(0, stations // step, fill, 0)


def make_weights(channels, beam_seeds, stations):
    slots = channels.shape[0]
    beams = beam_seeds.shape[0]
    return pl.pallas_call(
        functools.partial(weights_kernel, half_turn_fits()),
        grid=(slots,),
        in_specs=[
            pl.BlockSpec(memory_space=pltpu.SMEM),
            pl.BlockSpec((1, beams), lambda i: (0, 0)),
        ],
        out_specs=pl.BlockSpec((None, 2 * stations, 2 * beams), lambda i: (i, 0, 0)),
        out_shape=jax.ShapeDtypeStruct((slots, 2 * stations, 2 * beams), jnp.bfloat16),
        scratch_shapes=[pltpu.VMEM((stations, beams), jnp.float32)],
        cost_estimate=pl.CostEstimate(
            flops=slots * stations * beams * 40,
            bytes_accessed=slots * stations * beams * 8,
            transcendentals=0,
        ),
        name="steering_weights",
    )(channels, beam_seeds[None, :])


def split(values):
    high = values.astype(jnp.bfloat16)
    low = (values - high.astype(jnp.float32)).astype(jnp.bfloat16)
    return high, low


def dot(a, b, dims=(((1,), (0,)), ((), ()))):
    return lax.dot_general(a, b, dims, preferred_element_type=jnp.float32)


def inverse_factors(grams):
    rank = grams.shape[0]
    lanes = grams.shape[1]
    tall = 8
    blocks = rank // tall
    row = lax.broadcasted_iota(jnp.int32, (tall, lanes), 0)
    lane = lax.broadcasted_iota(jnp.int32, (tall, lanes), 1)
    inner = lax.rem(lane, rank)
    own = lane - inner
    pieces = [grams[tall * b : tall * (b + 1)] for b in range(blocks)]
    columns = [
        {
            b: jnp.take_along_axis(pieces[b], own + j, axis=1, mode="promise_in_bounds")
            for b in range(j // tall, blocks)
        }
        for j in range(rank)
    ]
    inverse = [jnp.where(inner == row + tall * b, 1.0, 0.0) for b in range(blocks)]
    scale = [jnp.ones((tall, lanes), jnp.float32) for _ in range(blocks)]

    def line(values, index):
        return jnp.broadcast_to(values[index : index + 1], (tall, lanes))

    for k in range(rank):
        at, inside = k // tall, k % tall
        column = columns[k]
        pivot = line(column[at], inside)
        scale[at] = jnp.where(row == inside, lax.rsqrt(pivot), scale[at])
        reciprocal = 1.0 / pivot
        factor = {b: column[b] * reciprocal for b in range(at, blocks)}
        factor[at] = jnp.where(row > inside, factor[at], 0.0)
        for j in range(k + 1, rank):
            entry = line(column[j // tall], j % tall)
            for b in range(j // tall, blocks):
                columns[j][b] = columns[j][b] - factor[b] * entry
        entry = line(inverse[at], inside)
        for b in range(at, blocks):
            inverse[b] = inverse[b] - factor[b] * entry
    return jnp.concatenate([inverse[b] * scale[b] for b in range(blocks)], axis=0)


def track_kernel(x_ref, state_ref, weight_any, beams_ref, new_ref, weight_ref, own_ref, direct_ref, sems):
    sources, parts, rows, signals = x_ref.shape
    slots, rank, _ = state_ref.shape
    times = rows // slots
    total = sources * times
    owners, _, _, mine, _ = beams_ref.shape
    images = weight_ref.shape[2]
    wide = 256
    cuts = range(0, images, wide)
    loads = []
    for j in range(slots):
        loads.append(pltpu.make_async_copy(weight_any.at[j], weight_ref.at[j], sems.at[j]))
        loads[-1].start()
    for j in range(slots):
        for part in range(parts):
            block = x_ref[:, part, times * j : times * (j + 1), :]
            own_ref[j, total * part : total * (part + 1), :] = block.reshape(total, signals)
    states = [state_ref[j] for j in range(slots)]
    vectors, shares = [], []
    for part in range(parts):
        span = slice(total * part, total * (part + 1))
        pairs, grams = [], []
        for j in range(slots):
            x = own_ref[j, span]
            y = dot(states[j].astype(jnp.bfloat16), x, NT).astype(jnp.bfloat16)
            high, low = split(dot(y, x) + float(total) * states[j])
            both = jnp.concatenate([high, low], axis=0)
            products = dot(both, both, NT)
            gram = products[:rank, :rank] + products[rank:, rank:]
            grams.append(gram + products[:rank, rank:] + products[rank:, :rank])
            pairs.append((high, low))
        if part == 0:
            for j in range(slots):
                loads[j].wait()
                for cut in cuts:
                    weight = weight_ref[j, :, cut : cut + wide]
                    direct_ref[j, :, cut : cut + wide] = dot(own_ref[j], weight)
        factors = inverse_factors(jnp.concatenate(grams, axis=1))
        for j in range(slots):
            high, low = pairs[j]
            left, under = split(factors[:, rank * j : rank * (j + 1)])
            states[j] = dot(left, high) + (dot(left, low) + dot(under, high))
        vectors.append([state.astype(jnp.bfloat16) for state in states])
        shares.append(
            [dot(own_ref[j, span], vectors[part][j], NT).astype(jnp.bfloat16) for j in range(slots)]
        )
    for j in range(slots):
        new_ref[j] = states[j]
        stack = jnp.concatenate([vectors[part][j] for part in range(parts)], axis=0)
        for cut in cuts:
            mixing = dot(stack, weight_ref[j, :, cut : cut + wide]).astype(jnp.bfloat16)
            for part in range(parts):
                removed = dot(shares[part][j], mixing[rank * part : rank * (part + 1)])
                formed = direct_ref[j, total * part : total * (part + 1), cut : cut + wide] - removed
                turned = formed.T.astype(jnp.bfloat16).reshape(wide // mine, mine, total)
                lead = cut // mine
                beams_ref[lead : lead + wide // mine, part, j] = turned


def track(x, state, weight, owners):
    slots, rank, signals = state.shape
    sources, parts, rows, _ = x.shape
    total = sources * rows // slots
    images = weight.shape[2]
    flops = 2 * parts * slots * total * signals * (images + 4 * rank)
    vmem = pl.BlockSpec(memory_space=pltpu.VMEM)
    hbm = pl.BlockSpec(memory_space=pltpu.HBM)
    beams = (owners, parts, slots, images // owners, total)
    return pl.pallas_call(
        track_kernel,
        in_specs=[vmem, vmem, hbm],
        out_specs=[vmem, vmem],
        out_shape=[
            jax.ShapeDtypeStruct(beams, jnp.bfloat16),
            jax.ShapeDtypeStruct(state.shape, jnp.float32),
        ],
        scratch_shapes=[
            pltpu.VMEM(weight.shape, jnp.bfloat16),
            pltpu.VMEM((slots, parts * total, signals), jnp.bfloat16),
            pltpu.VMEM((slots, parts * total, images), jnp.float32),
            pltpu.SemaphoreType.DMA((slots,)),
        ],
        compiler_params=pltpu.CompilerParams(vmem_limit_bytes=TRACK_LIMIT),
        cost_estimate=pl.CostEstimate(flops=flops, bytes_accessed=8 * MIB, transcendentals=0),
        name="track_and_form",
    )(x, state, weight)


def order_kernel(x_ref, out_any, sems):
    copies = []
    for part in range(out_any.shape[0]):
        copies.append(pltpu.make_async_copy(x_ref.at[:, part], out_any.at[part], sems.at[part]))
        copies[-1].start()
    for copy in copies:
        copy.wait()


def by_part(x):
    owners, parts, *rest = x.shape
    return pl.pallas_call(
        order_kernel,
        in_specs=[pl.BlockSpec(memory_space=pltpu.VMEM)],
        out_specs=pl.BlockSpec(memory_space=pltpu.HBM),
        out_shape=jax.ShapeDtypeStruct((parts, owners, *rest), x.dtype),
        scratch_shapes=[pltpu.SemaphoreType.DMA((parts,))],
        compiler_params=pltpu.CompilerParams(vmem_limit_bytes=16 * MIB),
        name="order_parts",
    )(x)


def per_device(voltages, subspace, order, beam_seeds, flagged):
    signals = voltages.shape[-1]
    slots = subspace.shape[1]
    per_group = order.shape[0]
    blocks = per_group // slots
    owners = lax.axis_size("chan")
    group = lax.axis_index("chan")
    chosen = lax.dynamic_slice_in_dim(order, lax.axis_index("tm") * slots, slots)
    channels = group * per_group + chosen
    picked = select(voltages, order, flagged, blocks)
    turned = lax.all_to_all(picked, "tm", split_axis=0, concat_axis=0, tiled=True)
    weight = make_weights(channels, beam_seeds, signals // 2)
    formed, state = track(turned, subspace[0], weight, owners)
    beams = lax.all_to_all(formed, "chan", split_axis=0, concat_axis=0, tiled=True)
    return (by_part(beams), state[None])


def solution(mesh):
    return jax.shard_map(
        per_device,
        mesh=mesh,
        in_specs=(P(None, "tm", "chan", None), P("chan", "tm", None, None), P(), P(), P()),
        out_specs=(P(None, None, "tm", "chan", None), P("chan", "tm", None, None)),
        check_vma=False,
    )
```

time: 213 us -> 141 us (0.66)
  the two profiles are of different devices: /device:TPU:18 before, /device:TPU:12 now
where the time goes in v1:
time: 141 us
  blocking collectives  71.6 us (51%)
  waiting for transfers between devices  37.6 us (27%)
  Pallas kernels  21.9 us (16%)
  starting transfers between devices  8.89 us (6%)
    all_to_all x1, blocking collectives, per_device(): lax.all_to_all(formed, 'chan', split_axis=0, concat_axis=0, tiled=True)  71.6 us
    all_to_all x1, waiting for transfers between devices, per_device(): lax.all_to_all(picked, 'tm', split_axis=0, concat_axis=0, tiled=True)  37.6 us
    pallas_call x1, Pallas kernels, track(): pl.pallas_call(track_kernel, in_specs=[vmem, vmem, hbm], out_specs=[vmem,...  10 us
    all_to_all x1, starting transfers between devices, per_device(): lax.all_to_all(picked, 'tm', split_axis=0, concat_axis=0, tiled=True)  8.89 us
    pallas_call x1, Pallas kernels, make_weights(): pl.pallas_call(functools.partial(weights_kernel, half_turn_fits()), grid=...  5.63 us
    pallas_call x1, Pallas kernels, select(): pl.pallas_call(select_kernel, in_specs=[hbm] * 3, out_specs=hbm, out_shap...  5.28 us
  transfers between devices with their start and end apart: 1, of which 1 were waited for; matrix products, arithmetic and copies ran while one was open for 0% of the time, Pallas kernels for 4%

profile of v1, /device:TPU:12, one launch (start us, length us, event | category | flops | bytes accessed | tf_op | source)
XLA Modules:
  0.0 141.3 jit_solution(3798738053604049270)
XLA Ops:
  0.6 5.3 %select_slots.1 = bf16[16,2,32,1024]{3,2,1,0:T(8,128)(2,1)} custom-call(s32[64]{0:T(128)} %order_any.1, s32[16]{0:T(128)} %flagged_any.1, bf16[2,8,64,1024]{3,2,1,0:T(8,128)(2,1)} %x_any.1), custom_call_target="tpu_custom_call" | custom-call | flops 1073741824 | bytes 4194304 | tf_op jit(solution)/shard_map/select_slots/pallas_call | solution.py:99
  5.9 0.0 copy-start.1
  5.9 8.9 %all-to-all-start = ((bf16[16,2,32,1024]{3,2,1,0:T(8,128)(2,1)}), bf16[16,2,32,1024]{3,2,1,0:T(8,128)(2,1)S(1)}, u32[]{:S(2)}, u32[]{:S(2)}) async-start(bf16[16,2,32,1024]{3,2,1,0:T(8,128)(2,1)} %select_slots.1), calls=%async_computation | async-start | bytes 4194304 | tf_op jit(solution)/shard_map/all_to_all | solution.py:366
  14.8 0.0 copy-done.1
  14.8 0.6 dynamic-slice_add_fusion.channel_ref
  15.4 0.0 copy-start
  15.4 5.6 %steering_weights.1.weight_any = bf16[4,1024,512]{2,1,0:T(8,128)(2,1)} custom-call(s32[4]{0:T(128)} %dynamic-slice_add_fusion.channel_ref, s32[1,256]{1,0:T(1,128)} %bitcast.4), custom_call_target="tpu_custom_call" | custom-call | flops 20971520 | bytes 4194304 | tf_op jit(solution)/shard_map/steering_weights/pallas_call | solution.py:176
  21.0 37.6 %all-to-all-done.x_ref = bf16[16,2,32,1024]{3,2,1,0:T(8,128)(2,1)S(1)} async-done(((bf16[16,2,32,1024]{3,2,1,0:T(8,128)(2,1)}), bf16[16,2,32,1024]{3,2,1,0:T(8,128)(2,1)S(1)}, u32[]{:S(2)}, u32[]{:S(2)}) %all-to-all-start) | async-done | bytes 2097184 | tf_op jit(solution)/shard_map/all_to_all | solution.py:366
  58.6 0.0 copy-done
  58.6 10.0 %track_and_form.1 = (bf16[32,2,4,16,128]{4,3,2,1,0:T(8,128)(2,1)S(1)}, f32[4,32,1024]{2,1,0:T(8,128)}) custom-call(bf16[16,2,32,1024]{3,2,1,0:T(8,128)(2,1)S(1)} %all-to-all-done.x_ref, f32[4,32,1024]{2,1,0:T(8,128)S(1)} %bitcast.3, bf16[4,1024,512]{2,1,0:T(8,128)(2,1)} %steering_weights.1.weight_any), custom_call_target="tpu_custom_call" | custom-call | flops 1342177280 | bytes 8388608 | tf_op jit(solution)/shard_map/track_and_form/pallas_call | solution.py:314
  68.7 71.6 %all_to_all.10.x_ref = bf16[32,2,4,16,128]{4,3,2,1,0:T(8,128)(2,1)S(1)} all-to-all(bf16[32,2,4,16,128]{4,3,2,1,0:T(8,128)(2,1)S(1)} %get-tuple-element.4), channel_id=1, replica_groups=mesh['tm'=16,'chan'=32] {'chan'}, dimensions={0} | all-to-all | bytes 2097152 | tf_op jit(solution)/shard_map/all_to_all | solution.py:369
  140.3 1.0 order_parts.1
Async XLA Ops:
  5.9 8.9 %copy-start.1 = (s32[64]{0:T(128)S(1)}, s32[64]{0:T(128)}, u32[]{:S(2)}) copy-start(s32[64]{0:T(128)} %order_any.1) | copy-start | bytes 772
  5.9 52.7 %all-to-all-start = ((bf16[16,2,32,1024]{3,2,1,0:T(8,128)(2,1)}), bf16[16,2,32,1024]{3,2,1,0:T(8,128)(2,1)S(1)}, u32[]{:S(2)}, u32[]{:S(2)}) async-start(bf16[16,2,32,1024]{3,2,1,0:T(8,128)(2,1)} %select_slots.1), calls=%async_computation | async-start | bytes 4194304 | tf_op jit(solution)/shard_map/all_to_all | solution.py:366
  15.4 43.2 %copy-start = (f32[1,4,32,1024]{3,2,1,0:T(8,128)S(1)}, f32[1,4,32,1024]{3,2,1,0:T(8,128)}, u32[]{:S(2)}) copy-start(f32[1,4,32,1024]{3,2,1,0:T(8,128)} %param.6) | copy-start | bytes 1572868

commit v2 on v1

--- a/solution.py
+++ b/solution.py
@@ -38,8 +38,8 @@
     owners, _, each, _ = out_any.shape
     rows = times * per_group
     stations = signals // 2
-    wide = signals // in_sems.shape[1]
-    cuts = [(p, c) for p in range(parts) for c in range(in_sems.shape[1])]
+    wide = 256
+    halves = out_sems.shape[1]
     small = [
         pltpu.make_async_copy(order_any, order_ref, small_sems.at[0]),
         pltpu.make_async_copy(flagged_any, flagged_ref, small_sems.at[1]),
@@ -47,13 +47,8 @@
     for copy in small:
         copy.start()
     loads = []
-    for p, c in cuts:
-        cut = pl.ds(c * wide, wide)
-        loads.append(
-            pltpu.make_async_copy(
-                x_any.at[p, :, :, cut], x_ref.at[p, :, :, cut], in_sems.at[p, c]
-            )
-        )
+    for p in range(parts):
+        loads.append(pltpu.make_async_copy(x_any.at[p], x_ref.at[p], in_sems.at[p]))
         loads[-1].start()
     for copy in small:
         copy.wait()
@@ -72,20 +67,20 @@
         dropped = jnp.logical_or(dropped, station == flagged_ref[entry])
     keep = jnp.where(dropped, 0.0, 1.0)
     stores = []
-    for (p, c), load in zip(cuts, loads, strict=True):
-        load.wait()
-        cut = slice(c * wide, (c + 1) * wide)
-        block = x_ref[p, :, :, cut].reshape(rows, wide)
-        moved = jnp.dot(pick_ref[...], block, preferred_element_type=jnp.float32)
-        moved = (moved * keep[0:1, cut]).astype(jnp.bfloat16)
-        out_ref[:, p, :, cut] = moved.reshape(owners, each, wide)
-        span = pl.ds(c * wide, wide)
-        stores.append(
-            pltpu.make_async_copy(
-                out_ref.at[:, p, :, span], out_any.at[:, p, :, span], out_sems.at[p, c]
-            )
-        )
-        stores[-1].start()
+    for p in range(parts):
+        loads[p].wait()
+        for h in range(halves):
+            lead = pl.ds(h * owners // halves, owners // halves)
+            taken = pick_ref[h * rows // halves : (h + 1) * rows // halves, :]
+            for start in range(0, signals, wide):
+                cut = slice(start, start + wide)
+                block = x_ref[p, :, :, cut].reshape(rows, wide)
+                moved = jnp.dot(taken, block, preferred_element_type=jnp.float32)
+                moved = (moved * keep[0:1, cut]).astype(jnp.bfloat16)
+                out_ref[lead, p, :, cut] = moved.reshape(owners // halves, each, wide)
+            target = out_any.at[lead, p]
+            stores.append(pltpu.make_async_copy(out_ref.at[lead, p], target, out_sems.at[p, h]))
+            stores[-1].start()
     for store in stores:
         store.wait()
 
@@ -93,7 +88,6 @@
 def select(voltages, order, flagged, owners):
     parts, times, per_group, signals = voltages.shape
     rows = times * per_group
-    cuts = 4
     hbm = pl.BlockSpec(memory_space=pltpu.HBM)
     shape = (owners, parts, rows // owners, signals)
     return pl.pallas_call(
@@ -108,8 +102,8 @@
             pltpu.VMEM((rows, rows), jnp.bfloat16),
             pltpu.VMEM(shape, jnp.bfloat16),
             pltpu.SemaphoreType.DMA((2,)),
-            pltpu.SemaphoreType.DMA((parts, cuts)),
-            pltpu.SemaphoreType.DMA((parts, cuts)),
+            pltpu.SemaphoreType.DMA((parts,)),
+            pltpu.SemaphoreType.DMA((parts, 2)),
         ],
         compiler_params=pltpu.CompilerParams(vmem_limit_bytes=67043328),
         cost_estimate=pl.CostEstimate(
@@ -243,7 +237,8 @@
     return jnp.concatenate([inverse[b] * scale[b] for b in range(blocks)], axis=0)
 
 
-def track_kernel(x_ref, state_ref, weight_any, beams_ref, new_ref, weight_ref, own_ref, direct_ref, sems):
+def track_kernel(x_ref, state_ref, weight_any, beams_ref, new_any, *scratch):
+    weight_ref, own_ref, direct_ref, new_ref, sems, new_sem = scratch
     sources, parts, rows, signals = x_ref.shape
     slots, rank, _ = state_ref.shape
     times = rows // slots
@@ -255,7 +250,9 @@
     loads = []
     for j in range(slots):
         loads.append(pltpu.make_async_copy(weight_any.at[j], weight_ref.at[j], sems.at[j]))
-        loads[-1].start()
+    for part in range(parts):
+        for j in range(part, slots, parts):
+            loads[j].start()
     for j in range(slots):
         for part in range(parts):
             block = x_ref[:, part, times * j : times * (j + 1), :]
@@ -274,8 +271,8 @@
             gram = products[:rank, :rank] + products[rank:, rank:]
             grams.append(gram + products[:rank, rank:] + products[rank:, :rank])
             pairs.append((high, low))
-        if part == 0:
-            for j in range(slots):
+        for j in range(slots):
+            if j % parts == part:
                 loads[j].wait()
                 for cut in cuts:
                     weight = weight_ref[j, :, cut : cut + wide]
@@ -285,12 +282,15 @@
             high, low = pairs[j]
             left, under = split(factors[:, rank * j : rank * (j + 1)])
             states[j] = dot(left, high) + (dot(left, low) + dot(under, high))
+            if part == parts - 1:
+                new_ref[j] = states[j]
         vectors.append([state.astype(jnp.bfloat16) for state in states])
         shares.append(
             [dot(own_ref[j, span], vectors[part][j], NT).astype(jnp.bfloat16) for j in range(slots)]
         )
+    leave = pltpu.make_async_copy(new_ref, new_any, new_sem)
+    leave.start()
     for j in range(slots):
-        new_ref[j] = states[j]
         stack = jnp.concatenate([vectors[part][j] for part in range(parts)], axis=0)
         for cut in cuts:
             mixing = dot(stack, weight_ref[j, :, cut : cut + wide]).astype(jnp.bfloat16)
@@ -300,6 +300,7 @@
                 turned = formed.T.astype(jnp.bfloat16).reshape(wide // mine, mine, total)
                 lead = cut // mine
                 beams_ref[lead : lead + wide // mine, part, j] = turned
+    leave.wait()
 
 
 def track(x, state, weight, owners):
@@ -314,7 +315,7 @@
     return pl.pallas_call(
         track_kernel,
         in_specs=[vmem, vmem, hbm],
-        out_specs=[vmem, vmem],
+        out_specs=[vmem, hbm],
         out_shape=[
             jax.ShapeDtypeStruct(beams, jnp.bfloat16),
             jax.ShapeDtypeStruct(state.shape, jnp.float32),
@@ -323,7 +324,9 @@
             pltpu.VMEM(weight.shape, jnp.bfloat16),
             pltpu.VMEM((slots, parts * total, signals), jnp.bfloat16),
             pltpu.VMEM((slots, parts * total, images), jnp.float32),
+            pltpu.VMEM(state.shape, jnp.float32),
             pltpu.SemaphoreType.DMA((slots,)),
+            pltpu.SemaphoreType.DMA,
         ],
         compiler_params=pltpu.CompilerParams(vmem_limit_bytes=TRACK_LIMIT),
         cost_estimate=pl.CostEstimate(flops=flops, bytes_accessed=8 * MIB, transcendentals=0),

time: 141 us -> 139 us (0.986)
  Pallas kernels: 21.9 us -> 19.6 us
    pallas_call x1, Pallas kernels: 5.28 us -> 3.55 us  [select(): pl.pallas_call(select_kernel, in_specs=[hbm] * 3, out_specs=hbm, out_shap...]
where the time goes in v2:
time: 139 us
  blocking collectives  71.6 us (52%)
  waiting for transfers between devices  37.6 us (27%)
  Pallas kernels  19.6 us (14%)
  starting transfers between devices  8.89 us (6%)
    all_to_all x1, blocking collectives, per_device(): lax.all_to_all(formed, 'chan', split_axis=0, concat_axis=0, tiled=True)  71.6 us
    all_to_all x1, waiting for transfers between devices, per_device(): lax.all_to_all(picked, 'tm', split_axis=0, concat_axis=0, tiled=True)  37.6 us
    pallas_call x1, Pallas kernels, track(): pl.pallas_call(track_kernel, in_specs=[vmem, vmem, hbm], out_specs=[vmem,...  9.43 us
    all_to_all x1, starting transfers between devices, per_device(): lax.all_to_all(picked, 'tm', split_axis=0, concat_axis=0, tiled=True)  8.89 us
    pallas_call x1, Pallas kernels, make_weights(): pl.pallas_call(functools.partial(weights_kernel, half_turn_fits()), grid=...  5.63 us
    pallas_call x1, Pallas kernels, select(): pl.pallas_call(select_kernel, in_specs=[hbm] * 3, out_specs=hbm, out_shap...  3.55 us
  transfers between devices with their start and end apart: 1, of which 1 were waited for; matrix products, arithmetic and copies ran while one was open for 0% of the time, Pallas kernels for 4%

profile of v2, /device:TPU:12, one launch (start us, length us, event | category | flops | bytes accessed | tf_op | source)
XLA Modules:
  0.0 138.9 jit_solution(9138991187983223089)
XLA Ops:
  0.6 3.6 %select_slots.1 = bf16[16,2,32,1024]{3,2,1,0:T(8,128)(2,1)} custom-call(s32[64]{0:T(128)} %order_any.1, s32[16]{0:T(128)} %flagged_any.1, bf16[2,8,64,1024]{3,2,1,0:T(8,128)(2,1)} %x_any.1), custom_call_target="tpu_custom_call" | custom-call | flops 1073741824 | bytes 4194304 | tf_op jit(solution)/shard_map/select_slots/pallas_call | solution.py:93
  4.2 0.0 copy-start.1
  4.2 8.9 %all-to-all-start = ((bf16[16,2,32,1024]{3,2,1,0:T(8,128)(2,1)}), bf16[16,2,32,1024]{3,2,1,0:T(8,128)(2,1)S(1)}, u32[]{:S(2)}, u32[]{:S(2)}) async-start(bf16[16,2,32,1024]{3,2,1,0:T(8,128)(2,1)} %select_slots.1), calls=%async_computation | async-start | bytes 4194304 | tf_op jit(solution)/shard_map/all_to_all | solution.py:369
  13.1 0.0 copy-done.1
  13.1 0.6 dynamic-slice_add_fusion.channel_ref
  13.7 0.0 copy-start
  13.7 5.6 %steering_weights.1.weight_any = bf16[4,1024,512]{2,1,0:T(8,128)(2,1)} custom-call(s32[4]{0:T(128)} %dynamic-slice_add_fusion.channel_ref, s32[1,256]{1,0:T(1,128)} %bitcast.4), custom_call_target="tpu_custom_call" | custom-call | flops 20971520 | bytes 4194304 | tf_op jit(solution)/shard_map/steering_weights/pallas_call | solution.py:170
  19.3 37.6 %all-to-all-done.x_ref = bf16[16,2,32,1024]{3,2,1,0:T(8,128)(2,1)S(1)} async-done(((bf16[16,2,32,1024]{3,2,1,0:T(8,128)(2,1)}), bf16[16,2,32,1024]{3,2,1,0:T(8,128)(2,1)S(1)}, u32[]{:S(2)}, u32[]{:S(2)}) %all-to-all-start) | async-done | bytes 2097184 | tf_op jit(solution)/shard_map/all_to_all | solution.py:369
  56.9 0.0 copy-done
  56.9 9.4 %track_and_form.1 = (bf16[32,2,4,16,128]{4,3,2,1,0:T(8,128)(2,1)S(1)}, f32[4,32,1024]{2,1,0:T(8,128)}) custom-call(bf16[16,2,32,1024]{3,2,1,0:T(8,128)(2,1)S(1)} %all-to-all-done.x_ref, f32[4,32,1024]{2,1,0:T(8,128)S(1)} %bitcast.3, bf16[4,1024,512]{2,1,0:T(8,128)(2,1)} %steering_weights.1.weight_any), custom_call_target="tpu_custom_call" | custom-call | flops 1342177280 | bytes 8388608 | tf_op jit(solution)/shard_map/track_and_form/pallas_call | solution.py:315
  66.3 71.6 %all_to_all.10.x_ref = bf16[32,2,4,16,128]{4,3,2,1,0:T(8,128)(2,1)S(1)} all-to-all(bf16[32,2,4,16,128]{4,3,2,1,0:T(8,128)(2,1)S(1)} %get-tuple-element.4), channel_id=1, replica_groups=mesh['tm'=16,'chan'=32] {'chan'}, dimensions={0} | all-to-all | bytes 2097152 | tf_op jit(solution)/shard_map/all_to_all | solution.py:372
  138.0 1.0 order_parts.1
Async XLA Ops:
  4.2 8.9 %copy-start.1 = (s32[64]{0:T(128)S(1)}, s32[64]{0:T(128)}, u32[]{:S(2)}) copy-start(s32[64]{0:T(128)} %order_any.1) | copy-start | bytes 772
  4.2 52.7 %all-to-all-start = ((bf16[16,2,32,1024]{3,2,1,0:T(8,128)(2,1)}), bf16[16,2,32,1024]{3,2,1,0:T(8,128)(2,1)S(1)}, u32[]{:S(2)}, u32[]{:S(2)}) async-start(bf16[16,2,32,1024]{3,2,1,0:T(8,128)(2,1)} %select_slots.1), calls=%async_computation | async-start | bytes 4194304 | tf_op jit(solution)/shard_map/all_to_all | solution.py:369
  13.7 43.2 %copy-start = (f32[1,4,32,1024]{3,2,1,0:T(8,128)S(1)}, f32[1,4,32,1024]{3,2,1,0:T(8,128)}, u32[]{:S(2)}) copy-start(f32[1,4,32,1024]{3,2,1,0:T(8,128)} %param.6) | copy-start | bytes 1572868

commit v3 on v2

--- a/solution.py
+++ b/solution.py
@@ -245,7 +245,7 @@
     total = sources * times
     owners, _, _, mine, _ = beams_ref.shape
     images = weight_ref.shape[2]
-    wide = 256
+    wide = 512
     cuts = range(0, images, wide)
     loads = []
     for j in range(slots):

time: 139 us -> 138 us (level)
  no operation moved by 1% of the time
where the time goes in v3:
time: 138 us
  blocking collectives  71.7 us (52%)
  waiting for transfers between devices  37.6 us (27%)
  Pallas kernels  18.6 us (13%)
  starting transfers between devices  8.89 us (6%)
    all_to_all x1, blocking collectives, per_device(): lax.all_to_all(formed, 'chan', split_axis=0, concat_axis=0, tiled=True)  71.7 us
    all_to_all x1, waiting for transfers between devices, per_device(): lax.all_to_all(picked, 'tm', split_axis=0, concat_axis=0, tiled=True)  37.6 us
    all_to_all x1, starting transfers between devices, per_device(): lax.all_to_all(picked, 'tm', split_axis=0, concat_axis=0, tiled=True)  8.89 us
    pallas_call x1, Pallas kernels, track(): pl.pallas_call(track_kernel, in_specs=[vmem, vmem, hbm], out_specs=[vmem,...  8.49 us
    pallas_call x1, Pallas kernels, make_weights(): pl.pallas_call(functools.partial(weights_kernel, half_turn_fits()), grid=...  5.63 us
    pallas_call x1, Pallas kernels, select(): pl.pallas_call(select_kernel, in_specs=[hbm] * 3, out_specs=hbm, out_shap...  3.55 us
  transfers between devices with their start and end apart: 1, of which 1 were waited for; matrix products, arithmetic and copies ran while one was open for 0% of the time, Pallas kernels for 4%

profile of v3, /device:TPU:12, one launch (start us, length us, event | category | flops | bytes accessed | tf_op | source)
XLA Modules:
  0.0 138.0 jit_solution(3605416237297534398)
XLA Ops:
  0.6 3.6 %select_slots.1 = bf16[16,2,32,1024]{3,2,1,0:T(8,128)(2,1)} custom-call(s32[64]{0:T(128)} %order_any.1, s32[16]{0:T(128)} %flagged_any.1, bf16[2,8,64,1024]{3,2,1,0:T(8,128)(2,1)} %x_any.1), custom_call_target="tpu_custom_call" | custom-call | flops 1073741824 | bytes 4194304 | tf_op jit(solution)/shard_map/select_slots/pallas_call | solution.py:93
  4.2 0.0 copy-start.1
  4.2 8.9 %all-to-all-start = ((bf16[16,2,32,1024]{3,2,1,0:T(8,128)(2,1)}), bf16[16,2,32,1024]{3,2,1,0:T(8,128)(2,1)S(1)}, u32[]{:S(2)}, u32[]{:S(2)}) async-start(bf16[16,2,32,1024]{3,2,1,0:T(8,128)(2,1)} %select_slots.1), calls=%async_computation | async-start | bytes 4194304 | tf_op jit(solution)/shard_map/all_to_all | solution.py:369
  13.1 0.0 copy-done.1
  13.1 0.6 dynamic-slice_add_fusion.channel_ref
  13.7 0.0 copy-start
  13.7 5.6 %steering_weights.1.weight_any = bf16[4,1024,512]{2,1,0:T(8,128)(2,1)} custom-call(s32[4]{0:T(128)} %dynamic-slice_add_fusion.channel_ref, s32[1,256]{1,0:T(1,128)} %bitcast.4), custom_call_target="tpu_custom_call" | custom-call | flops 20971520 | bytes 4194304 | tf_op jit(solution)/shard_map/steering_weights/pallas_call | solution.py:170
  19.3 37.6 %all-to-all-done.x_ref = bf16[16,2,32,1024]{3,2,1,0:T(8,128)(2,1)S(1)} async-done(((bf16[16,2,32,1024]{3,2,1,0:T(8,128)(2,1)}), bf16[16,2,32,1024]{3,2,1,0:T(8,128)(2,1)S(1)}, u32[]{:S(2)}, u32[]{:S(2)}) %all-to-all-start) | async-done | bytes 2097184 | tf_op jit(solution)/shard_map/all_to_all | solution.py:369
  56.9 0.0 copy-done
  56.9 8.5 %track_and_form.1 = (bf16[32,2,4,16,128]{4,3,2,1,0:T(8,128)(2,1)S(1)}, f32[4,32,1024]{2,1,0:T(8,128)}) custom-call(bf16[16,2,32,1024]{3,2,1,0:T(8,128)(2,1)S(1)} %all-to-all-done.x_ref, f32[4,32,1024]{2,1,0:T(8,128)S(1)} %bitcast.3, bf16[4,1024,512]{2,1,0:T(8,128)(2,1)} %steering_weights.1.weight_any), custom_call_target="tpu_custom_call" | custom-call | flops 1342177280 | bytes 8388608 | tf_op jit(solution)/shard_map/track_and_form/pallas_call | solution.py:315
  65.4 71.7 %all_to_all.10.x_ref = bf16[32,2,4,16,128]{4,3,2,1,0:T(8,128)(2,1)S(1)} all-to-all(bf16[32,2,4,16,128]{4,3,2,1,0:T(8,128)(2,1)S(1)} %get-tuple-element.4), channel_id=1, replica_groups=mesh['tm'=16,'chan'=32] {'chan'}, dimensions={0} | all-to-all | bytes 2097152 | tf_op jit(solution)/shard_map/all_to_all | solution.py:372
  137.1 1.0 order_parts.1
Async XLA Ops:
  4.2 8.9 %copy-start.1 = (s32[64]{0:T(128)S(1)}, s32[64]{0:T(128)}, u32[]{:S(2)}) copy-start(s32[64]{0:T(128)} %order_any.1) | copy-start | bytes 772
  4.2 52.7 %all-to-all-start = ((bf16[16,2,32,1024]{3,2,1,0:T(8,128)(2,1)}), bf16[16,2,32,1024]{3,2,1,0:T(8,128)(2,1)S(1)}, u32[]{:S(2)}, u32[]{:S(2)}) async-start(bf16[16,2,32,1024]{3,2,1,0:T(8,128)(2,1)} %select_slots.1), calls=%async_computation | async-start | bytes 4194304 | tf_op jit(solution)/shard_map/all_to_all | solution.py:369
  13.7 43.2 %copy-start = (f32[1,4,32,1024]{3,2,1,0:T(8,128)S(1)}, f32[1,4,32,1024]{3,2,1,0:T(8,128)}, u32[]{:S(2)}) copy-start(f32[1,4,32,1024]{3,2,1,0:T(8,128)} %param.6) | copy-start | bytes 1572868
